TPU v7x, 256 devices: a whole 4x4x8 slice. The times are simulated.
256 devices in a mesh: tm: 16 (over x_hi, y, core), space: 16 (over x_lo, z).
Axes of the slice: x: 4 (x_hi: 2, x_lo: 2; x = x_hi * 2 + x_lo), y: 4, z: 8, core: 2. Of those that a mesh axis runs over, the one named last changes fastest.
Arguments:
- gauge_links: float32 [16, 2, 3, 3, 3, 32, 1024], P('tm', None, None, None, None, 'space'), may hold values from -1 to 1, as said below
- time_links: float32 [16, 2, 3, 3, 32, 1024], P('tm', None, None, None, 'space'), may hold values from -1 to 1, as said below
- sink_vectors: bfloat16 [16, 2, 128, 3, 32, 1024], P('tm', None, None, None, 'space'), may hold values from -0.29882812 to 0.29882812
- source_times: int32 [4], replicated, may hold values from 0 to 15
- source_index: int32 [4, 2], replicated, may hold values from 0 to 127
- kinetic_coef: float32 [4, 2], replicated, may hold values from 0.005 to 0.12
Outputs:
- perambulator: float32 [2, 4, 2, 16, 128], P(None, None, None, 'tm', 'space')
Inputs may be any that keep to these rules, and one draw needn't show every extreme that they name: `gauge_links`: each link is a special unitary 3 x 3 matrix. `time_links`: each link is a special unitary 3 x 3 matrix.
All inputs are finite; a program needn't handle non-finite values.
Results may differ from a plain program's by a relative error of at most 0.0029.
Values may be sent and summed in bfloat16 or wider, within the bound.
A program may use at most 128 MiB of HBM per device.

v0:
```python
import functools

import jax
import jax.numpy as jnp
from jax import lax
from jax.experimental import pallas as pl
from jax.experimental.pallas import tpu as pltpu
from jax.sharding import PartitionSpec as P

MESH = pl.DeviceIdType.MESH
F32 = jnp.float32
BF16 = jnp.bfloat16
SLOTS = 4


def modulo(value, length):
    return jnp.where(value < 0, value + length, value)


def times(links, field):
    real, imag = None, None
    for b in range(3):
        u_re, u_im = links(0, slice(None), b), links(1, slice(None), b)
        f_re, f_im = field[0][b : b + 1], field[1][b : b + 1]
        re = u_re * f_re - u_im * f_im
        im = u_re * f_im + u_im * f_re
        real, imag = (re, im) if real is None else (real + re, imag + im)
    return real, imag


def adjoint_times(links, field):
    real, imag = None, None
    for b in range(3):
        u_re, u_im = links(0, b, slice(None)), links(1, b, slice(None))
        f_re, f_im = field[0][b : b + 1], field[1][b : b + 1]
        re = u_re * f_re + u_im * f_im
        im = u_re * f_im - u_im * f_re
        real, imag = (re, im) if real is None else (real + re, imag + im)
    return real, imag


def kernel(
    n_tm, n_space, rounds,
    times_ref, index_ref, coef_ref, gauge_hbm, temporal_hbm, sinks_hbm,
    out_ref,
    gauge_in, temporal_in, sinks, link_x, link_yz, link_t,
    up_out, down_out, low_links, high_links,
    staged, own_src, low_src, high_src,
    recv_own, recv_low, recv_high, sent_own, record,
    field, turned, chosen, summed, partial, parts,
    local_sem, halo_send, halo_recv, step_send, step_recv, part_send, part_recv,
):
    t = lax.axis_index("tm")
    i = lax.axis_index("space")
    after, before = lax.rem(t + 1, n_tm), lax.rem(t + n_tm - 1, n_tm)
    above, below = lax.rem(i + 1, n_space), lax.rem(i + n_space - 1, n_space)

    fetches = [
        pltpu.make_async_copy(gauge_hbm, gauge_in, local_sem.at[0]),
        pltpu.make_async_copy(temporal_hbm, temporal_in, local_sem.at[1]),
        pltpu.make_async_copy(sinks_hbm, sinks, local_sem.at[2]),
    ]
    for fetch in fetches:
        fetch.start()

    barrier = pltpu.get_barrier_semaphore()
    for near_t in (before, after):
        for near_i in (below, i, above):
            pl.semaphore_signal(
                barrier, inc=1, device_id={"tm": near_t, "space": near_i}, device_id_type=MESH
            )
    for step in range(1, n_space):
        pl.semaphore_signal(
            barrier, inc=1,
            device_id={"tm": t, "space": lax.rem(i + step, n_space)}, device_id_type=MESH,
        )

    recv_own[0] = jnp.zeros_like(recv_own[0])
    recv_low[0] = jnp.zeros_like(recv_low[0])
    recv_high[0] = jnp.zeros_like(recv_high[0])

    start = [times_ref[k] for k in range(SLOTS)]
    late, lane = [], []
    for k in range(SLOTS):
        free = []
        for d in range(SLOTS - 1):
            place = modulo(start[k] - d, n_tm)
            ok = jnp.int32(1)
            for other in lane:
                ok = jnp.where(other == place, 0, ok)
            free.append(ok)
        d = jnp.int32(SLOTS - 1)
        for value in reversed(range(SLOTS - 1)):
            d = jnp.where(free[value] == 1, value, d)
        late.append(d)
        lane.append(modulo(start[k] - d, n_tm))
    here, which = [], []
    for d in range(SLOTS):
        count = jnp.int32(0)
        index = [jnp.int32(0), jnp.int32(0)]
        for k in range(SLOTS):
            match = jnp.where(start[k] == t, jnp.where(late[k] == d, 1, 0), 0)
            count = count + match
            index = [index[j] + match * index_ref[k, j] for j in range(2)]
        here.append(count)
        which.append(index)

    fetches[0].wait()
    fetches[1].wait()
    for x in range(2):
        for row in range(3):
            for col in range(3):
                for mu in range(3):
                    pair = []
                    for ri in range(2):
                        plane = gauge_in[ri, mu, row, col, pl.ds(x, 8, stride=2), :]
                        pair.append(plane)
                        if mu == 0:
                            link_x[2 + x, ri, row, col] = plane
                        else:
                            link_yz[1 + x, mu - 1, ri, row, col] = plane
                    packed = jnp.concatenate(pair, axis=0).astype(BF16)
                    if x == 1:
                        up_out[(mu * 3 + row) * 3 + col] = packed
                    else:
                        down_out[(mu * 3 + row) * 3 + col] = packed
                        if mu == 0:
                            up_out[36 + row * 3 + col] = packed
                pair = []
                for ri in range(2):
                    plane = temporal_in[ri, row, col, pl.ds(x, 8, stride=2), :]
                    pair.append(plane)
                    link_t[1 + x, ri, row, col] = plane
                packed = jnp.concatenate(pair, axis=0).astype(BF16)
                if x == 1:
                    up_out[27 + row * 3 + col] = packed
                else:
                    down_out[27 + row * 3 + col] = packed

    fetches[2].wait()
    for d in range(SLOTS):
        keep = here[d].astype(F32)
        for j in range(2):
            for ri in range(2):
                for c in range(3):
                    staged[d, j, ri * 3 + c] = sinks[ri, which[d][j], c].astype(F32) * keep
    for d in range(SLOTS):
        for j in range(2):
            for part in range(6):
                planes = [staged[d, j, part, pl.ds(x, 8, stride=2), :] for x in range(2)]
                own_src[d, j, part] = jnp.concatenate(planes, axis=0).astype(BF16)

    pl.semaphore_wait(barrier, 6 + n_space - 1)

    def halo(number, src, dst, device):
        return pltpu.make_async_remote_copy(
            src_ref=src, dst_ref=dst, send_sem=halo_send.at[number], recv_sem=halo_recv.at[number],
            device_id={"tm": t, "space": device}, device_id_type=MESH,
        )

    source_halos = [
        (
            halo(2 * d, own_src.at[d], low_src.at[d], above),
            halo(2 * d + 1, own_src.at[d], high_src.at[d], below),
        )
        for d in range(SLOTS)
    ]
    link_halos = (
        halo(2 * SLOTS, up_out, low_links, above),
        halo(2 * SLOTS + 1, down_out, high_links, below),
    )
    for copy in link_halos + source_halos[0] + source_halos[1] + source_halos[2] + source_halos[3]:
        copy.start()

    link_halos[0].wait_recv()
    for row in range(3):
        for col in range(3):
            for mu in range(3):
                both = low_links[(mu * 3 + row) * 3 + col].astype(F32)
                for ri in range(2):
                    if mu == 0:
                        link_x[1, ri, row, col] = both[8 * ri : 8 * ri + 8]
                    else:
                        link_yz[0, mu - 1, ri, row, col] = both[8 * ri : 8 * ri + 8]
            both = low_links[27 + row * 3 + col].astype(F32)
            for ri in range(2):
                link_t[0, ri, row, col] = both[8 * ri : 8 * ri + 8]
            both = low_links[36 + row * 3 + col].astype(F32)
            for ri in range(2):
                link_x[0, ri, row, col] = both[8 * ri : 8 * ri + 8]
    link_halos[1].wait_recv()
    for row in range(3):
        for col in range(3):
            for mu in range(3):
                both = high_links[(mu * 3 + row) * 3 + col].astype(F32)
                for ri in range(2):
                    if mu == 0:
                        link_x[4, ri, row, col] = both[8 * ri : 8 * ri + 8]
                    else:
                        link_yz[3, mu - 1, ri, row, col] = both[8 * ri : 8 * ri + 8]
            both = high_links[27 + row * 3 + col].astype(F32)
            for ri in range(2):
                link_t[3, ri, row, col] = both[8 * ri : 8 * ri + 8]

    lanes = lax.broadcasted_iota(jnp.int32, (3, 8, 128), 2)
    z = lax.rem(lanes, 32)
    first_z, last_z = z == 0, z == 31
    low_lanes, high_lanes = lanes < 32, lanes >= 96

    def up(values, direction):
        if direction == 0:
            moved = pltpu.roll(values, 96, 2)
            return jnp.where(high_lanes, pltpu.roll(moved, 7, 1), moved)
        return jnp.where(last_z, pltpu.roll(values, 31, 2), pltpu.roll(values, 127, 2))

    def down(values, direction):
        if direction == 0:
            moved = pltpu.roll(values, 32, 2)
            return jnp.where(low_lanes, pltpu.roll(moved, 1, 1), moved)
        return jnp.where(first_z, pltpu.roll(values, 97, 2), pltpu.roll(values, 1, 2))

    def relaxed(source, q, links_q, weight):
        at = lambda p: (source[p, 0:3], source[p, 3:6])
        centre = at(q)
        re, im = times(lambda ri, a, b: link_x[links_q + 1, ri, a, b], at(q + 1))
        more = adjoint_times(lambda ri, a, b: link_x[links_q, ri, a, b], at(q - 1))
        re, im = re + more[0], im + more[1]
        for direction in range(2):
            links = lambda ri, a, b: link_yz[links_q, direction, ri, a, b]
            more = times(links, tuple(up(part, direction) for part in centre))
            re, im = re + more[0], im + more[1]
            more = tuple(down(part, direction) for part in adjoint_times(links, centre))
            re, im = re + more[0], im + more[1]
        rest = 1.0 - 6.0 * weight
        return rest * centre[0] + weight * re, rest * centre[1] + weight * im

    def hop(number, device_t, r, j):
        if number == 0:
            src, dst, target = record.at[r, j], recv_low.at[r + 1, j], above
        elif number == 1:
            src, dst, target = record.at[r, j], recv_high.at[r + 1, j], below
        else:
            src, dst, target = sent_own.at[r, j], recv_own.at[r + 1, j], i
        return pltpu.make_async_remote_copy(
            src_ref=src, dst_ref=dst,
            send_sem=step_send.at[r, j, number], recv_sem=step_recv.at[r, j, number],
            device_id={"tm": device_t, "space": target}, device_id_type=MESH,
        )

    def one_source(n, carry):
        r, j = n // 2, lax.rem(n, 2)
        for d in range(SLOTS):

            @pl.when(n == 2 * d)
            def _():
                for copy in source_halos[d]:
                    copy.wait_recv()

        @pl.when(r > 0)
        def _():
            for number in range(3):
                hop(number, after, r - 1, j).wait_recv()

        @pl.when(r < SLOTS)
        def _():
            d = jnp.minimum(r, SLOTS - 1)
            take = jnp.where(r == 0, 1, 0)
            for late_by in range(1, SLOTS):
                take = jnp.where(r == late_by, here[late_by], take)
            inject = jnp.full((16, 128), take, jnp.int32) > 0
            for part in range(6):
                arrived = jnp.concatenate([recv_own[r, j, x, part] for x in range(2)], axis=0)
                for place, begun, came in (
                    (0, low_src, recv_low[r, j, part].astype(F32)),
                    (2, own_src, arrived),
                    (4, high_src, recv_high[r, j, part].astype(F32)),
                ):
                    value = jnp.where(inject, begun[d, j, part].astype(F32), came)
                    field[place, part] = value[0:8]
                    field[place + 1, part] = value[8:16]

        @pl.when(r >= SLOTS)
        def _():
            for part in range(6):
                for place, came in ((0, recv_low), (4, recv_high)):
                    value = came[r, j, part].astype(F32)
                    field[place, part] = value[0:8]
                    field[place + 1, part] = value[8:16]
                for x in range(2):
                    field[2 + x, part] = recv_own[r, j, x, part]

        on_lane = lax.rem(t - r + 2 * n_tm, n_tm)
        weight = jnp.float32(0)
        for k in range(SLOTS):
            weight = jnp.where(lane[k] == on_lane, 0.5 * coef_ref[k, j], weight)

        for q in range(4):
            half = relaxed(field, q + 1, q, weight)
            re, im = adjoint_times(lambda ri, a, b: link_t[q, ri, a, b], half)
            turned[q, 0:3] = re
            turned[q, 3:6] = im
        results = []
        for x in range(2):
            re, im = relaxed(turned, x + 1, x + 1, weight)
            sent_own[r, j, x, 0:3] = re
            sent_own[r, j, x, 3:6] = im
            results.append((re, im))
        for ri in range(2):
            both = jnp.concatenate([results[0][ri], results[1][ri]], axis=1)
            record[r, j, 3 * ri : 3 * ri + 3] = both.astype(BF16)

        @pl.when(r < rounds - 1)
        def _():
            for number in range(3):
                hop(number, after, r, j).start()

        return carry

    lax.fori_loop(0, 2 * rounds, one_source, 0)

    for k in range(SLOTS):
        round_of = late[k] + modulo(t - start[k], n_tm)
        for j in range(2):
            for ri in range(2):
                for c in range(3):
                    spot = ((k * 2 + j) * 2 + ri) * 16
                    chosen[c, spot : spot + 16] = record[round_of, j, ri * 3 + c]
    row = lax.broadcasted_iota(jnp.int32, (16, 256), 0)
    col = lax.rem(lax.broadcasted_iota(jnp.int32, (16, 256), 1), 16)
    same = jnp.where(row == 2 * lax.rem(col, 8) + col // 8, 1.0, 0.0).astype(F32)
    n_sinks = sinks.shape[1]

    def some_sinks(step, carry):
        first = pl.multiple_of(step * 16, 16)
        for ri in range(2):
            products = None
            for c in range(3):
                block = sinks[ri, pl.ds(first, 16), c].reshape(256, 128)
                product = lax.dot_general(
                    block, chosen[c], (((1,), (1,)), ((), ())), preferred_element_type=F32
                )
                products = product if products is None else products + product
            products = products.reshape(16, 16, 256) * same[None]
            summed[ri, pl.ds(first, 16), :] = jnp.sum(products, axis=1)
        return carry

    lax.fori_loop(0, n_sinks // 16, some_sinks, 0)
    entry = lax.broadcasted_iota(jnp.int32, (256, 128), 0) // 16
    column = lax.broadcasted_iota(jnp.int32, (256, 128), 1)
    field_ri, field_v = lax.rem(entry, 2), entry // 2
    from_re = jnp.where(column == field_ri * 8 + field_v, 1.0, 0.0)
    from_im = jnp.where(column == (1 - field_ri) * 8 + field_v, 1.0, 0.0)
    from_im = from_im * jnp.where(field_ri == 1, 1.0, -1.0)
    partial[...] = jnp.dot(
        summed[0], from_re.astype(F32), precision=lax.Precision.HIGHEST, preferred_element_type=F32
    ) + jnp.dot(
        summed[1], from_im.astype(F32), precision=lax.Precision.HIGHEST, preferred_element_type=F32
    )

    share = n_sinks // n_space

    def give(step):
        target = lax.rem(i + step, n_space)
        return pltpu.make_async_remote_copy(
            src_ref=partial.at[pl.ds(pl.multiple_of(target * share, share), share)],
            dst_ref=parts.at[step],
            send_sem=part_send.at[step], recv_sem=part_recv.at[step],
            device_id={"tm": t, "space": target}, device_id_type=MESH,
        )

    for step in range(1, n_space):
        give(step).start()
    total = partial[pl.ds(pl.multiple_of(i * share, share), share), :]
    for step in range(1, n_space):
        give(step).wait_recv()
        total = total + parts[step]
    out_ref[...] = total

    for step in range(1, n_space):
        give(step).wait_send()
    for copy in link_halos + source_halos[0] + source_halos[1] + source_halos[2] + source_halos[3]:
        copy.wait_send()

    def finish(n, carry):
        for number in range(3):
            hop(number, after, n // 2, lax.rem(n, 2)).wait_send()
        return carry

    lax.fori_loop(0, 2 * (rounds - 1), finish, 0)


def rows_of(x):
    lead = x.shape[:-2]
    x = x.reshape(*lead, 2, 8, 128)
    x = jnp.swapaxes(x, x.ndim - 3, x.ndim - 2)
    return x.reshape(*lead, 16, 128)


def local(gauge_links, time_links, sink_vectors, source_times, source_index, kinetic_coef):
    n_tm, n_space = lax.axis_size("tm"), lax.axis_size("space")
    n_sinks = sink_vectors.shape[2]
    rounds = n_tm + SLOTS - 1
    share = n_sinks // n_space
    smem = pl.BlockSpec(memory_space=pltpu.SMEM)
    hbm = pl.BlockSpec(memory_space=pl.ANY)
    vmem = pltpu.VMEM
    dma = pltpu.SemaphoreType.DMA
    result = pl.pallas_call(
        functools.partial(kernel, n_tm, n_space, rounds),
        out_shape=jax.ShapeDtypeStruct((share, 128), F32),
        in_specs=[smem, smem, smem, hbm, hbm, hbm],
        out_specs=pl.BlockSpec(memory_space=pltpu.VMEM),
        scratch_shapes=[
            vmem((2, 3, 3, 3, 16, 128), F32),
            vmem((2, 3, 3, 16, 128), F32),
            vmem((2, n_sinks, 3, 16, 128), BF16),
            vmem((5, 2, 3, 3, 8, 128), F32),
            vmem((4, 2, 2, 3, 3, 8, 128), F32),
            vmem((4, 2, 3, 3, 8, 128), F32),
            vmem((45, 16, 128), BF16),
            vmem((36, 16, 128), BF16),
            vmem((45, 16, 128), BF16),
            vmem((36, 16, 128), BF16),
            vmem((SLOTS, 2, 6, 16, 128), F32),
            vmem((SLOTS, 2, 6, 16, 128), BF16),
            vmem((SLOTS, 2, 6, 16, 128), BF16),
            vmem((SLOTS, 2, 6, 16, 128), BF16),
            vmem((rounds, 2, 2, 6, 8, 128), F32),
            vmem((rounds, 2, 6, 16, 128), BF16),
            vmem((rounds, 2, 6, 16, 128), BF16),
            vmem((rounds, 2, 2, 6, 8, 128), F32),
            vmem((rounds, 2, 6, 16, 128), BF16),
            vmem((6, 6, 8, 128), F32),
            vmem((4, 6, 8, 128), F32),
            vmem((3, 256, 128), BF16),
            vmem((2, n_sinks, 256), F32),
            vmem((n_sinks, 128), F32),
            vmem((n_space, share, 128), F32),
            dma((3,)),
            dma((2 * SLOTS + 2,)),
            dma((2 * SLOTS + 2,)),
            dma((rounds - 1, 2, 3)),
            dma((rounds - 1, 2, 3)),
            dma((n_space,)),
            dma((n_space,)),
        ],
        compiler_params=pltpu.CompilerParams(collective_id=0, has_side_effects=True),
    )(
        source_times, source_index, kinetic_coef,
        rows_of(gauge_links[0]), rows_of(time_links[0]), rows_of(sink_vectors[0]),
    )
    groups, per_group = kinetic_coef.shape
    table = result[:, : 2 * groups * per_group].reshape(share, 2, groups, per_group)
    return jnp.moveaxis(table, 0, 3)[:, :, :, None, :]


def solution(mesh):
    placed = (
        P("tm", None, None, None, None, "space", None),
        P("tm", None, None, None, "space", None),
        P("tm", None, None, None, "space", None),
        P(),
        P(),
        P(),
    )
    return jax.shard_map(
        local,
        mesh=mesh,
        in_specs=placed,
        out_specs=P(None, None, None, "tm", "space"),
        check_vma=False,
    )
```

profile of v0, /device:TPU:1, one launch (start us, length us, event | category | flops | bytes accessed | tf_op | source)
XLA Modules:
  0.0 115.0 jit_solution(10230140534862668541)
XLA Ops:
  0.0 1.3 %copy.10.index_ref = s32[4,2]{1,0:T(4,128)} copy(s32[4,2]{0,1:T(2,128)} %param.10) | data formatting | bytes 64 | tf_op args[4]
  1.3 1.3 %copy.11.coef_ref = f32[4,2]{1,0:T(4,128)} copy(f32[4,2]{0,1:T(2,128)} %param.11) | data formatting | bytes 64 | tf_op args[5]
  2.7 110.9 %shard_map.64 = f32[8,128]{1,0:T(8,128)} custom-call(s32[4]{0:T(128)} %times_ref.1, s32[4,2]{1,0:T(4,128)} %copy.10.index_ref, f32[4,2]{1,0:T(4,128)} %copy.11.coef_ref, f32[2,3,3,3,16,128]{5,4,3,2,1,0:T(8,128)} %bitcast.24, f32[2,3,3,16,128]{4,3,2,1,0:T(8,128)} %bitcast.25, bf16[2,128,3,16,128]{4,3,2,1,0:T(8,128)(2,1)} %bitcast.23), custom_call_target="tpu_custom_call" | custom-call | tf_op jit(solution)/shard_map/pallas_call | solution.py:408
  113.6 1.4 %copy.12 = f32[8,16]{0,1:T(8,128)} copy(f32[8,16]{1,0:T(8,128)} %bitcast.26) | data formatting | bytes 1024 | tf_op jit(solution)/shard_map/slice | solution.py:453
where the time goes:
time: 115 us
  Pallas kernels  111 us (97%)
  local copies, waits for them, and re-layouts  4.03 us (4%)
    pallas_call x1, Pallas kernels, local(): pl.pallas_call(functools.partial(kernel, n_tm, n_space, rounds), out_shap...  111 us
    unnamed x2, local copies, waits for them, and re-layouts  2.68 us

commit v1 on v0

v1 whole, which is shorter than its diff:
```python
import functools

import jax
import jax.numpy as jnp
from jax import lax
from jax.experimental import pallas as pl
from jax.experimental.pallas import tpu as pltpu
from jax.sharding import PartitionSpec as P

MESH = pl.DeviceIdType.MESH
F32 = jnp.float32
BF16 = jnp.bfloat16
SLOTS = 4


def modulo(value, length):
    return jnp.where(value < 0, value + length, value)


def schedule(start, n_tm):
    late, lane = [], []
    for k in range(SLOTS):
        free = []
        for d in range(SLOTS - 1):
            place = modulo(start[k] - d, n_tm)
            ok = jnp.int32(1)
            for other in lane:
                ok = jnp.where(other == place, 0, ok)
            free.append(ok)
        d = jnp.int32(SLOTS - 1)
        for value in reversed(range(SLOTS - 1)):
            d = jnp.where(free[value] == 1, value, d)
        late.append(d)
        lane.append(modulo(start[k] - d, n_tm))
    return late, lane


def times(links, field):
    real, imag = None, None
    for b in range(3):
        u_re, u_im = links(0, slice(None), b), links(1, slice(None), b)
        f_re, f_im = field[0][b : b + 1], field[1][b : b + 1]
        re = u_re * f_re - u_im * f_im
        im = u_re * f_im + u_im * f_re
        real, imag = (re, im) if real is None else (real + re, imag + im)
    return real, imag


def adjoint_times(links, field):
    real, imag = None, None
    for b in range(3):
        u_re, u_im = links(0, b, slice(None)), links(1, b, slice(None))
        f_re, f_im = field[0][b : b + 1], field[1][b : b + 1]
        re = u_re * f_re + u_im * f_im
        im = u_re * f_im - u_im * f_re
        real, imag = (re, im) if real is None else (real + re, imag + im)
    return real, imag


def kernel(
    n_tm, n_space, slots,
    times_ref, index_ref, coef_ref, gauge_hbm, temporal_hbm, sinks_hbm,
    out_ref,
    gauge_in, temporal_in, sinks, link_x, link_yz, link_t,
    up_out, down_out, low_links, high_links,
    staged, own_src, low_src, high_src,
    recv_own, recv_low, recv_high, sent_own, record,
    field, turned, chosen, summed, partial, parts,
    local_sem, halo_send, halo_recv, step_send, step_recv, part_send, part_recv,
):
    rounds = n_tm + slots - 1
    t = lax.axis_index("tm")
    i = lax.axis_index("space")
    after, before = lax.rem(t + 1, n_tm), lax.rem(t + n_tm - 1, n_tm)
    above, below = lax.rem(i + 1, n_space), lax.rem(i + n_space - 1, n_space)

    fetches = [
        pltpu.make_async_copy(gauge_hbm, gauge_in, local_sem.at[0]),
        pltpu.make_async_copy(temporal_hbm, temporal_in, local_sem.at[1]),
        pltpu.make_async_copy(sinks_hbm, sinks, local_sem.at[2]),
    ]
    for fetch in fetches:
        fetch.start()

    barrier = pltpu.get_barrier_semaphore()
    for near_t in (before, after):
        for near_i in (below, i, above):
            pl.semaphore_signal(
                barrier, inc=1, device_id={"tm": near_t, "space": near_i}, device_id_type=MESH
            )
    for step in range(1, n_space):
        pl.semaphore_signal(
            barrier, inc=1,
            device_id={"tm": t, "space": lax.rem(i + step, n_space)}, device_id_type=MESH,
        )

    recv_own[0] = jnp.zeros_like(recv_own[0])
    recv_low[0] = jnp.zeros_like(recv_low[0])
    recv_high[0] = jnp.zeros_like(recv_high[0])

    start = [times_ref[k] for k in range(SLOTS)]
    late, lane = schedule(start, n_tm)
    here, which = [], []
    for d in range(SLOTS):
        count = jnp.int32(0)
        index = [jnp.int32(0), jnp.int32(0)]
        for k in range(SLOTS):
            match = jnp.where(start[k] == t, jnp.where(late[k] == d, 1, 0), 0)
            count = count + match
            index = [index[j] + match * index_ref[j, k] for j in range(2)]
        here.append(count)
        which.append(index)

    fetches[0].wait()
    fetches[1].wait()
    for x in range(2):
        for row in range(3):
            for col in range(3):
                for mu in range(4):
                    pair = []
                    for ri in range(2):
                        if mu == 3:
                            plane = temporal_in[ri, row, col, pl.ds(x, 8, stride=2), :]
                            link_t[1 + x, ri, row, col] = plane
                        else:
                            plane = gauge_in[ri, mu, row, col, pl.ds(x, 8, stride=2), :]
                            if mu == 0:
                                link_x[2 + x, ri, row, col] = plane
                            else:
                                link_yz[1 + x, mu - 1, ri, row, col] = plane
                        pair.append(plane)
                    if row < 2:
                        packed = jnp.concatenate(pair, axis=0).astype(BF16)
                        if x == 1:
                            up_out[mu, row * 3 + col] = packed
                        else:
                            down_out[mu, row * 3 + col] = packed
                            if mu == 0:
                                up_out[4, row * 3 + col] = packed

    pl.semaphore_wait(barrier, 6 + n_space - 1)

    def halo(number, src, dst, device):
        return pltpu.make_async_remote_copy(
            src_ref=src, dst_ref=dst, send_sem=halo_send.at[number], recv_sem=halo_recv.at[number],
            device_id={"tm": t, "space": device}, device_id_type=MESH,
        )

    link_halos = (
        halo(2 * SLOTS, up_out, low_links, above),
        halo(2 * SLOTS + 1, down_out, high_links, below),
    )
    for copy in link_halos:
        copy.start()

    fetches[2].wait()
    source_halos = []
    for d in range(slots):
        keep = here[d].astype(F32)
        for j in range(2):
            for ri in range(2):
                for c in range(3):
                    staged[d, j, ri * 3 + c] = sinks[ri, which[d][j], c].astype(F32) * keep
            for part in range(6):
                planes = [staged[d, j, part, pl.ds(x, 8, stride=2), :] for x in range(2)]
                own_src[d, j, part] = jnp.concatenate(planes, axis=0).astype(BF16)
        source_halos.append(
            (
                halo(2 * d, own_src.at[d], low_src.at[d], above),
                halo(2 * d + 1, own_src.at[d], high_src.at[d], below),
            )
        )
        for copy in source_halos[d]:
            copy.start()

    def unpack(packed, store):
        rows = [[packed[row * 3 + col].astype(F32) for col in range(3)] for row in range(2)]
        re = [[entry[0:8] for entry in row] for row in rows]
        im = [[entry[8:16] for entry in row] for row in rows]
        last_re, last_im = [], []
        for col in range(3):
            a, b = (col + 1) % 3, (col + 2) % 3
            last_re.append(
                (re[0][a] * re[1][b] - im[0][a] * im[1][b]) - (re[0][b] * re[1][a] - im[0][b] * im[1][a])
            )
            last_im.append(
                (re[0][b] * im[1][a] + im[0][b] * re[1][a]) - (re[0][a] * im[1][b] + im[0][a] * re[1][b])
            )
        re, im = re + [last_re], im + [last_im]
        for row in range(3):
            for col in range(3):
                store[0, row, col] = re[row][col]
                store[1, row, col] = im[row][col]

    link_halos[0].wait_recv()
    link_halos[1].wait_recv()
    for arrived, x_plane, plane in ((low_links, 1, 0), (high_links, 4, 3)):
        unpack(arrived.at[0], link_x.at[x_plane])
        unpack(arrived.at[1], link_yz.at[plane, 0])
        unpack(arrived.at[2], link_yz.at[plane, 1])
        unpack(arrived.at[3], link_t.at[plane])
    unpack(low_links.at[4], link_x.at[0])

    lanes = lax.broadcasted_iota(jnp.int32, (3, 8, 128), 2)
    z = lax.rem(lanes, 32)
    first_z, last_z = z == 0, z == 31
    low_lanes, high_lanes = lanes < 32, lanes >= 96

    def up(values, direction):
        if direction == 0:
            moved = pltpu.roll(values, 96, 2)
            return jnp.where(high_lanes, pltpu.roll(moved, 7, 1), moved)
        return jnp.where(last_z, pltpu.roll(values, 31, 2), pltpu.roll(values, 127, 2))

    def down(values, direction):
        if direction == 0:
            moved = pltpu.roll(values, 32, 2)
            return jnp.where(low_lanes, pltpu.roll(moved, 1, 1), moved)
        return jnp.where(first_z, pltpu.roll(values, 97, 2), pltpu.roll(values, 1, 2))

    def relaxed(source, q, links_q, weight):
        at = lambda p: (source[p, 0:3], source[p, 3:6])
        centre = at(q)
        re, im = times(lambda ri, a, b: link_x[links_q + 1, ri, a, b], at(q + 1))
        more = adjoint_times(lambda ri, a, b: link_x[links_q, ri, a, b], at(q - 1))
        re, im = re + more[0], im + more[1]
        for direction in range(2):
            links = lambda ri, a, b: link_yz[links_q, direction, ri, a, b]
            more = times(links, tuple(up(part, direction) for part in centre))
            re, im = re + more[0], im + more[1]
            more = tuple(down(part, direction) for part in adjoint_times(links, centre))
            re, im = re + more[0], im + more[1]
        rest = 1.0 - 6.0 * weight
        return rest * centre[0] + weight * re, rest * centre[1] + weight * im

    def hop(number, device_t, r, j):
        if number == 0:
            src, dst, target = record.at[r, j], recv_low.at[r + 1, j], above
        elif number == 1:
            src, dst, target = record.at[r, j], recv_high.at[r + 1, j], below
        else:
            src, dst, target = sent_own.at[r, j], recv_own.at[r + 1, j], i
        return pltpu.make_async_remote_copy(
            src_ref=src, dst_ref=dst,
            send_sem=step_send.at[r, j, number], recv_sem=step_recv.at[r, j, number],
            device_id={"tm": device_t, "space": target}, device_id_type=MESH,
        )

    def one_source(n, carry):
        r, j = n // 2, lax.rem(n, 2)
        for d in range(slots):

            @pl.when(n == 2 * d)
            def _():
                for copy in source_halos[d]:
                    copy.wait_recv()

        @pl.when(r > 0)
        def _():
            for number in range(3):
                hop(number, after, r - 1, j).wait_recv()

        @pl.when(r < slots)
        def _():
            d = jnp.minimum(r, slots - 1)
            take = jnp.where(r == 0, 1, 0)
            for late_by in range(1, slots):
                take = jnp.where(r == late_by, here[late_by], take)
            inject = jnp.full((16, 128), take, jnp.int32) > 0
            for part in range(6):
                arrived = jnp.concatenate([recv_own[r, j, x, part] for x in range(2)], axis=0)
                for place, begun, came in (
                    (0, low_src, recv_low[r, j, part].astype(F32)),
                    (2, own_src, arrived),
                    (4, high_src, recv_high[r, j, part].astype(F32)),
                ):
                    value = jnp.where(inject, begun[d, j, part].astype(F32), came)
                    field[place, part] = value[0:8]
                    field[place + 1, part] = value[8:16]

        @pl.when(r >= slots)
        def _():
            for part in range(6):
                for place, came in ((0, recv_low), (4, recv_high)):
                    value = came[r, j, part].astype(F32)
                    field[place, part] = value[0:8]
                    field[place + 1, part] = value[8:16]
                for x in range(2):
                    field[2 + x, part] = recv_own[r, j, x, part]

        on_lane = lax.rem(t - r + 2 * n_tm, n_tm)
        weight = jnp.float32(0)
        for k in range(SLOTS):
            weight = jnp.where(lane[k] == on_lane, 0.5 * coef_ref[j, k], weight)

        for q in range(4):
            half = relaxed(field, q + 1, q, weight)
            re, im = adjoint_times(lambda ri, a, b: link_t[q, ri, a, b], half)
            turned[q, 0:3] = re
            turned[q, 3:6] = im
        results = []
        for x in range(2):
            re, im = relaxed(turned, x + 1, x + 1, weight)
            sent_own[r, j, x, 0:3] = re
            sent_own[r, j, x, 3:6] = im
            results.append((re, im))
        for ri in range(2):
            both = jnp.concatenate([results[0][ri], results[1][ri]], axis=1)
            record[r, j, 3 * ri : 3 * ri + 3] = both.astype(BF16)

        @pl.when(r < rounds - 1)
        def _():
            for number in range(3):
                hop(number, after, r, j).start()

        return carry

    lax.fori_loop(0, 2 * rounds, one_source, 0)

    for k in range(SLOTS):
        round_of = jnp.minimum(late[k] + modulo(t - start[k], n_tm), rounds - 1)
        for j in range(2):
            for c in range(3):
                spot = (k * 2 + j) * 16
                re, im = record[round_of, j, c], record[round_of, j, 3 + c]
                chosen[c, spot : spot + 16] = jnp.concatenate([re, im], axis=1)
                chosen[c, 128 + spot : 128 + spot + 16] = jnp.concatenate([im, -re], axis=1)
    row = lax.broadcasted_iota(jnp.int32, (16, 256), 0)
    col = lax.rem(lax.broadcasted_iota(jnp.int32, (16, 256), 1), 16)
    same = jnp.where(row == 2 * lax.rem(col, 8) + col // 8, 1.0, 0.0).astype(F32)
    n_sinks = sinks.shape[1]

    def some_sinks(step, carry):
        first = pl.multiple_of(step * 16, 16)
        products = None
        for c in range(3):
            block = jnp.concatenate([sinks[ri, pl.ds(first, 16), c].reshape(256, 128) for ri in range(2)], axis=1)
            product = lax.dot_general(
                block, chosen[c], (((1,), (1,)), ((), ())), preferred_element_type=F32
            )
            products = product if products is None else products + product
        products = products.reshape(16, 16, 256) * same[None]
        summed[pl.ds(first, 16), :] = jnp.sum(products, axis=1)
        return carry

    lax.fori_loop(0, n_sinks // 16, some_sinks, 0)
    entry = lax.broadcasted_iota(jnp.int32, (256, 128), 0) // 16
    column = lax.broadcasted_iota(jnp.int32, (256, 128), 1)
    fold = jnp.where(entry == column, 1.0, 0.0).astype(F32)
    partial[...] = jnp.dot(
        summed[...], fold, precision=lax.Precision.HIGHEST, preferred_element_type=F32
    )

    share = n_sinks // n_space

    def give(step):
        target = lax.rem(i + step, n_space)
        return pltpu.make_async_remote_copy(
            src_ref=partial.at[pl.ds(pl.multiple_of(target * share, share), share)],
            dst_ref=parts.at[step],
            send_sem=part_send.at[step], recv_sem=part_recv.at[step],
            device_id={"tm": t, "space": target}, device_id_type=MESH,
        )

    for step in range(1, n_space):
        give(step).start()
    total = partial[pl.ds(pl.multiple_of(i * share, share), share), :]
    for step in range(1, n_space):
        give(step).wait_recv()
        total = total + parts[step]
    out_ref[...] = total

    for step in range(1, n_space):
        give(step).wait_send()
    for copy in sum(source_halos, link_halos):
        copy.wait_send()

    def finish(n, carry):
        for number in range(3):
            hop(number, after, n // 2, lax.rem(n, 2)).wait_send()
        return carry

    lax.fori_loop(0, 2 * (rounds - 1), finish, 0)


def latest_start(n_tm, times_ref, out_ref):
    late, _ = schedule([times_ref[k] for k in range(SLOTS)], n_tm)
    latest = late[0]
    for d in late[1:]:
        latest = jnp.maximum(latest, d)
    out_ref[0] = latest


def rows_of(x):
    lead = x.shape[:-2]
    x = x.reshape(*lead, 2, 8, 128)
    x = jnp.swapaxes(x, x.ndim - 3, x.ndim - 2)
    return x.reshape(*lead, 16, 128)


def local(gauge_links, time_links, sink_vectors, source_times, source_index, kinetic_coef):
    n_tm, n_space = lax.axis_size("tm"), lax.axis_size("space")
    n_sinks = sink_vectors.shape[2]
    share = n_sinks // n_space
    smem = pl.BlockSpec(memory_space=pltpu.SMEM)
    hbm = pl.BlockSpec(memory_space=pl.ANY)
    vmem = pltpu.VMEM
    dma = pltpu.SemaphoreType.DMA

    def with_slots(slots):
        rounds = n_tm + slots - 1
        return pl.pallas_call(
            functools.partial(kernel, n_tm, n_space, slots),
            out_shape=jax.ShapeDtypeStruct((share, 128), F32),
            in_specs=[smem, smem, smem, hbm, hbm, hbm],
            out_specs=pl.BlockSpec(memory_space=pltpu.VMEM),
            scratch_shapes=[
                vmem((2, 3, 3, 3, 16, 128), F32),
                vmem((2, 3, 3, 16, 128), F32),
                vmem((2, n_sinks, 3, 16, 128), BF16),
                vmem((5, 2, 3, 3, 8, 128), F32),
                vmem((4, 2, 2, 3, 3, 8, 128), F32),
                vmem((4, 2, 3, 3, 8, 128), F32),
                vmem((5, 6, 16, 128), BF16),
                vmem((4, 6, 16, 128), BF16),
                vmem((5, 6, 16, 128), BF16),
                vmem((4, 6, 16, 128), BF16),
                vmem((slots, 2, 6, 16, 128), F32),
                vmem((slots, 2, 6, 16, 128), BF16),
                vmem((slots, 2, 6, 16, 128), BF16),
                vmem((slots, 2, 6, 16, 128), BF16),
                vmem((rounds, 2, 2, 6, 8, 128), F32),
                vmem((rounds, 2, 6, 16, 128), BF16),
                vmem((rounds, 2, 6, 16, 128), BF16),
                vmem((rounds, 2, 2, 6, 8, 128), F32),
                vmem((rounds, 2, 6, 16, 128), BF16),
                vmem((6, 6, 8, 128), F32),
                vmem((4, 6, 8, 128), F32),
                vmem((3, 256, 256), BF16),
                vmem((n_sinks, 256), F32),
                vmem((n_sinks, 128), F32),
                vmem((n_space, share, 128), F32),
                dma((3,)),
                dma((2 * SLOTS + 2,)),
                dma((2 * SLOTS + 2,)),
                dma((rounds - 1, 2, 3)),
                dma((rounds - 1, 2, 3)),
                dma((n_space,)),
                dma((n_space,)),
            ],
            compiler_params=pltpu.CompilerParams(collective_id=slots - 1, has_side_effects=True),
        )

    latest = pl.pallas_call(
        functools.partial(latest_start, n_tm),
        out_shape=jax.ShapeDtypeStruct((1,), jnp.int32),
        in_specs=[smem],
        out_specs=smem,
    )(source_times)[0]
    result = lax.switch(
        latest,
        [with_slots(slots) for slots in range(1, SLOTS + 1)],
        source_times, source_index.T, kinetic_coef.T,
        rows_of(gauge_links[0]), rows_of(time_links[0]), rows_of(sink_vectors[0]),
    )
    groups, per_group = kinetic_coef.shape
    table = result[:, : 2 * groups * per_group].reshape(share, 2, groups, per_group)
    return jnp.moveaxis(table, 0, 3)[:, :, :, None, :]


def solution(mesh):
    placed = (
        P("tm", None, None, None, None, "space", None),
        P("tm", None, None, None, "space", None),
        P("tm", None, None, None, "space", None),
        P(),
        P(),
        P(),
    )
    return jax.shard_map(
        local,
        mesh=mesh,
        in_specs=placed,
        out_specs=P(None, None, None, "tm", "space"),
        check_vma=False,
    )
```

time: 115 us -> 94.7 us (0.82)
  Pallas kernels: 111 us -> 93.2 us
  local copies, waits for them, and re-layouts: 4.03 us -> 0.67 us
    pallas_call x1 -> x2, Pallas kernels: 111 us -> 93.2 us  [the longest x1 92 us: local(): lax.switch(latest, [with_slots(slots) for slots in range(1, SLOTS + 1)],...]
    unnamed x2 -> x1, local copies, waits for them, and re-layouts: 2.68 us -> 0.67 us
    slice x1 -> x0, local copies, waits for them, and re-layouts: 1.35 us -> none  [local(): result[:, :2 * groups * per_group].reshape(share, 2, groups, per_group)]
where the time goes in v1:
time: 94.7 us; the launch traced here: 94.5 us
  Pallas kernels  93.2 us (98%)
    pallas_call x1, Pallas kernels, local(): lax.switch(latest, [with_slots(slots) for slots in range(1, SLOTS + 1)],...  92 us

profile of v1, /device:TPU:1, one launch (start us, length us, event | category | flops | bytes accessed | tf_op | source)
XLA Modules:
  0.0 94.5 jit_solution(11721330238595880192)
XLA Ops:
  0.0 1.2 %shard_map.64 = s32[1]{0:T(128)} custom-call(s32[4]{0:T(128)} %times_ref.1), custom_call_target="tpu_custom_call" | custom-call | tf_op jit(solution)/shard_map/pallas_call | solution.py:454
  1.9 92.0 %conditional.1 = (f32[8,128]{1,0:T(8,128)S(1)}) conditional(s32[]{:T(128)} %bitcast, (s32[4]{0:T(128)}, s32[2,4]{1,0:T(2,128)}, f32[2,4]{1,0:T(2,128)}, f32[2,3,3,3,16,128]{5,4,3,2,1,0:T(8,128)}, f32[2,3,3,16,128]{4,3,2,1,0:T(8,128)}, /*index=5*/bf16[2,128,3,16,128]{4,3,2,1,0:T(8,128)(2,1)}) %tuple.38, (s32[4]{0:T(128)}, ...), branch_computations={%region_0.0_spmd, %region_1.0_spmd, %region_2.0_spmd, %region_3.0_... | conditional | bytes 8 | solution.py:460
  1.9 92.0 %branch_0_fun.1 = f32[8,128]{1,0:T(8,128)S(1)} custom-call(s32[4]{0:T(128)} %get-tuple-element.56.times_ref, s32[2,4]{1,0:T(2,128)} %get-tuple-element.58.index_ref, f32[2,4]{1,0:T(2,128)} %get-tuple-element.60.coef_ref, f32[2,3,3,3,16,128]{5,4,3,2,1,0:T(8,128)} %get-tuple-element.61.gauge_hbm, f32[2,3,3,16,128]{4,3,2,1,0:T(8,128)} %get-tuple-element.62.temporal_hbm, ...), custom_call_target="tpu_custom_call" | custom-call | tf_op jit(solution)/shard_map/cond/branch_0_fun/pallas_call | solution.py:460
  93.9 0.7 copy.12

commit v2 on v1

--- a/solution.py
+++ b/solution.py
@@ -65,7 +65,7 @@
     up_out, down_out, low_links, high_links,
     staged, own_src, low_src, high_src,
     recv_own, recv_low, recv_high, sent_own, record,
-    field, turned, chosen, summed, partial, parts,
+    field, early, turned, chosen, summed, partial, parts,
     local_sem, halo_send, halo_recv, step_send, step_recv, part_send, part_recv,
 ):
     rounds = n_tm + slots - 1
@@ -218,20 +218,27 @@
             return jnp.where(low_lanes, pltpu.roll(moved, 1, 1), moved)
         return jnp.where(first_z, pltpu.roll(values, 97, 2), pltpu.roll(values, 1, 2))
 
-    def relaxed(source, q, links_q, weight):
+    def neighbours(source, q, links_q, total=None, x_up=True, x_down=True, flat=True):
         at = lambda p: (source[p, 0:3], source[p, 3:6])
-        centre = at(q)
-        re, im = times(lambda ri, a, b: link_x[links_q + 1, ri, a, b], at(q + 1))
-        more = adjoint_times(lambda ri, a, b: link_x[links_q, ri, a, b], at(q - 1))
-        re, im = re + more[0], im + more[1]
-        for direction in range(2):
-            links = lambda ri, a, b: link_yz[links_q, direction, ri, a, b]
-            more = times(links, tuple(up(part, direction) for part in centre))
-            re, im = re + more[0], im + more[1]
-            more = tuple(down(part, direction) for part in adjoint_times(links, centre))
-            re, im = re + more[0], im + more[1]
+
+        def plus(more):
+            return more if total is None else (total[0] + more[0], total[1] + more[1])
+
+        if flat:
+            centre = at(q)
+            for direction in range(2):
+                links = lambda ri, a, b: link_yz[links_q, direction, ri, a, b]
+                total = plus(times(links, tuple(up(part, direction) for part in centre)))
+                total = plus(tuple(down(part, direction) for part in adjoint_times(links, centre)))
+        if x_up:
+            total = plus(times(lambda ri, a, b: link_x[links_q + 1, ri, a, b], at(q + 1)))
+        if x_down:
+            total = plus(adjoint_times(lambda ri, a, b: link_x[links_q, ri, a, b], at(q - 1)))
+        return total
+
+    def relaxed(source, q, total, weight):
         rest = 1.0 - 6.0 * weight
-        return rest * centre[0] + weight * re, rest * centre[1] + weight * im
+        return rest * source[q, 0:3] + weight * total[0], rest * source[q, 3:6] + weight * total[1]
 
     def hop(number, device_t, r, j):
         if number == 0:
@@ -255,26 +262,46 @@
                 for copy in source_halos[d]:
                     copy.wait_recv()
 
+        d = jnp.minimum(r, slots - 1)
+        take = jnp.where(r == 0, 1, 0)
+        for late_by in range(1, slots):
+            take = jnp.where(r == late_by, here[late_by], take)
+
         @pl.when(r > 0)
         def _():
-            for number in range(3):
-                hop(number, after, r - 1, j).wait_recv()
+            hop(2, after, r - 1, j).wait_recv()
 
         @pl.when(r < slots)
         def _():
-            d = jnp.minimum(r, slots - 1)
-            take = jnp.where(r == 0, 1, 0)
-            for late_by in range(1, slots):
-                take = jnp.where(r == late_by, here[late_by], take)
             inject = jnp.full((16, 128), take, jnp.int32) > 0
             for part in range(6):
                 arrived = jnp.concatenate([recv_own[r, j, x, part] for x in range(2)], axis=0)
-                for place, begun, came in (
-                    (0, low_src, recv_low[r, j, part].astype(F32)),
-                    (2, own_src, arrived),
-                    (4, high_src, recv_high[r, j, part].astype(F32)),
-                ):
-                    value = jnp.where(inject, begun[d, j, part].astype(F32), came)
+                value = jnp.where(inject, own_src[d, j, part].astype(F32), arrived)
+                field[2, part] = value[0:8]
+                field[3, part] = value[8:16]
+
+        @pl.when(r >= slots)
+        def _():
+            for part in range(6):
+                for x in range(2):
+                    field[2 + x, part] = recv_own[r, j, x, part]
+
+        for q in (1, 2):
+            re, im = neighbours(field, q + 1, q, x_up=q == 1, x_down=q == 2)
+            early[q - 1, 0:3] = re
+            early[q - 1, 3:6] = im
+
+        @pl.when(r > 0)
+        def _():
+            for number in range(2):
+                hop(number, after, r - 1, j).wait_recv()
+
+        @pl.when(r < slots)
+        def _():
+            inject = jnp.full((16, 128), take, jnp.int32) > 0
+            for part in range(6):
+                for place, begun, came in ((0, low_src, recv_low), (4, high_src, recv_high)):
+                    value = jnp.where(inject, begun[d, j, part], came[r, j, part]).astype(F32)
                     field[place, part] = value[0:8]
                     field[place + 1, part] = value[8:16]
 
@@ -285,8 +312,6 @@
                     value = came[r, j, part].astype(F32)
                     field[place, part] = value[0:8]
                     field[place + 1, part] = value[8:16]
-                for x in range(2):
-                    field[2 + x, part] = recv_own[r, j, x, part]
 
         on_lane = lax.rem(t - r + 2 * n_tm, n_tm)
         weight = jnp.float32(0)
@@ -294,13 +319,20 @@
             weight = jnp.where(lane[k] == on_lane, 0.5 * coef_ref[j, k], weight)
 
         for q in range(4):
-            half = relaxed(field, q + 1, q, weight)
+            if q == 0 or q == 3:
+                total = neighbours(field, q + 1, q)
+            else:
+                total = neighbours(
+                    field, q + 1, q, (early[q - 1, 0:3], early[q - 1, 3:6]),
+                    x_up=q == 2, x_down=q == 1, flat=False,
+                )
+            half = relaxed(field, q + 1, total, weight)
             re, im = adjoint_times(lambda ri, a, b: link_t[q, ri, a, b], half)
             turned[q, 0:3] = re
             turned[q, 3:6] = im
         results = []
         for x in range(2):
-            re, im = relaxed(turned, x + 1, x + 1, weight)
+            re, im = relaxed(turned, x + 1, neighbours(turned, x + 1, x + 1), weight)
             sent_own[r, j, x, 0:3] = re
             sent_own[r, j, x, 3:6] = im
             results.append((re, im))
@@ -331,19 +363,19 @@
     n_sinks = sinks.shape[1]
 
     def some_sinks(step, carry):
-        first = pl.multiple_of(step * 16, 16)
+        first = pl.multiple_of(step * 64, 64)
         products = None
         for c in range(3):
-            block = jnp.concatenate([sinks[ri, pl.ds(first, 16), c].reshape(256, 128) for ri in range(2)], axis=1)
+            block = jnp.concatenate([sinks[ri, pl.ds(first, 64), c].reshape(1024, 128) for ri in range(2)], axis=1)
             product = lax.dot_general(
                 block, chosen[c], (((1,), (1,)), ((), ())), preferred_element_type=F32
             )
             products = product if products is None else products + product
-        products = products.reshape(16, 16, 256) * same[None]
-        summed[pl.ds(first, 16), :] = jnp.sum(products, axis=1)
+        products = products.reshape(64, 16, 256) * same[None]
+        summed[pl.ds(first, 64), :] = jnp.sum(products, axis=1)
         return carry
 
-    lax.fori_loop(0, n_sinks // 16, some_sinks, 0)
+    lax.fori_loop(0, n_sinks // 64, some_sinks, 0, unroll=False)
     entry = lax.broadcasted_iota(jnp.int32, (256, 128), 0) // 16
     column = lax.broadcasted_iota(jnp.int32, (256, 128), 1)
     fold = jnp.where(entry == column, 1.0, 0.0).astype(F32)
@@ -435,6 +467,7 @@
                 vmem((rounds, 2, 2, 6, 8, 128), F32),
                 vmem((rounds, 2, 6, 16, 128), BF16),
                 vmem((6, 6, 8, 128), F32),
+                vmem((2, 6, 8, 128), F32),
                 vmem((4, 6, 8, 128), F32),
                 vmem((3, 256, 256), BF16),
                 vmem((n_sinks, 256), F32),

time: 94.7 us -> 92 us (0.971)
  Pallas kernels: 93.2 us -> 90.5 us
    pallas_call x1, Pallas kernels: 92 us -> 89.3 us  [local(): lax.switch(latest, [with_slots(slots) for slots in range(1, SLOTS + 1)],...]
where the time goes in v2:
time: 92 us; the launch traced here: 91.8 us
  Pallas kernels  90.5 us (98%)
    pallas_call x1, Pallas kernels, local(): lax.switch(latest, [with_slots(slots) for slots in range(1, SLOTS + 1)],...  89.3 us

profile of v2, /device:TPU:1, one launch (start us, length us, event | category | flops | bytes accessed | tf_op | source)
XLA Modules:
  0.0 91.8 jit_solution(5911730625513065996)
XLA Ops:
  0.0 1.2 %shard_map.64 = s32[1]{0:T(128)} custom-call(s32[4]{0:T(128)} %times_ref.1), custom_call_target="tpu_custom_call" | custom-call | tf_op jit(solution)/shard_map/pallas_call | solution.py:487
  1.9 89.3 %conditional.1 = (f32[8,128]{1,0:T(8,128)S(1)}) conditional(s32[]{:T(128)} %bitcast, (s32[4]{0:T(128)}, s32[2,4]{1,0:T(2,128)}, f32[2,4]{1,0:T(2,128)}, f32[2,3,3,3,16,128]{5,4,3,2,1,0:T(8,128)}, f32[2,3,3,16,128]{4,3,2,1,0:T(8,128)}, /*index=5*/bf16[2,128,3,16,128]{4,3,2,1,0:T(8,128)(2,1)}) %tuple.38, (s32[4]{0:T(128)}, ...), branch_computations={%region_0.0_spmd, %region_1.0_spmd, %region_2.0_spmd, %region_3.0_... | conditional | bytes 8 | solution.py:493
  1.9 89.3 %branch_0_fun.1 = f32[8,128]{1,0:T(8,128)S(1)} custom-call(s32[4]{0:T(128)} %get-tuple-element.56.times_ref, s32[2,4]{1,0:T(2,128)} %get-tuple-element.58.index_ref, f32[2,4]{1,0:T(2,128)} %get-tuple-element.60.coef_ref, f32[2,3,3,3,16,128]{5,4,3,2,1,0:T(8,128)} %get-tuple-element.61.gauge_hbm, f32[2,3,3,16,128]{4,3,2,1,0:T(8,128)} %get-tuple-element.62.temporal_hbm, ...), custom_call_target="tpu_custom_call" | custom-call | tf_op jit(solution)/shard_map/cond/branch_0_fun/pallas_call | solution.py:493
  91.2 0.7 copy.12

commit v3 on v2

--- a/solution.py
+++ b/solution.py
@@ -192,9 +192,11 @@
                 store[0, row, col] = re[row][col]
                 store[1, row, col] = im[row][col]
 
-    link_halos[0].wait_recv()
-    link_halos[1].wait_recv()
-    for arrived, x_plane, plane in ((low_links, 1, 0), (high_links, 4, 3)):
+    for arrived, copy, x_plane, plane in (
+        (high_links, link_halos[1], 4, 3),
+        (low_links, link_halos[0], 1, 0),
+    ):
+        copy.wait_recv()
         unpack(arrived.at[0], link_x.at[x_plane])
         unpack(arrived.at[1], link_yz.at[plane, 0])
         unpack(arrived.at[2], link_yz.at[plane, 1])
@@ -255,13 +257,6 @@
 
     def one_source(n, carry):
         r, j = n // 2, lax.rem(n, 2)
-        for d in range(slots):
-
-            @pl.when(n == 2 * d)
-            def _():
-                for copy in source_halos[d]:
-                    copy.wait_recv()
-
         d = jnp.minimum(r, slots - 1)
         take = jnp.where(r == 0, 1, 0)
         for late_by in range(1, slots):
@@ -291,45 +286,52 @@
             early[q - 1, 0:3] = re
             early[q - 1, 3:6] = im
 
-        @pl.when(r > 0)
-        def _():
-            for number in range(2):
-                hop(number, after, r - 1, j).wait_recv()
-
-        @pl.when(r < slots)
-        def _():
-            inject = jnp.full((16, 128), take, jnp.int32) > 0
-            for part in range(6):
-                for place, begun, came in ((0, low_src, recv_low), (4, high_src, recv_high)):
-                    value = jnp.where(inject, begun[d, j, part], came[r, j, part]).astype(F32)
-                    field[place, part] = value[0:8]
-                    field[place + 1, part] = value[8:16]
-
-        @pl.when(r >= slots)
-        def _():
-            for part in range(6):
-                for place, came in ((0, recv_low), (4, recv_high)):
-                    value = came[r, j, part].astype(F32)
-                    field[place, part] = value[0:8]
-                    field[place + 1, part] = value[8:16]
-
         on_lane = lax.rem(t - r + 2 * n_tm, n_tm)
         weight = jnp.float32(0)
         for k in range(SLOTS):
             weight = jnp.where(lane[k] == on_lane, 0.5 * coef_ref[j, k], weight)
 
-        for q in range(4):
-            if q == 0 or q == 3:
-                total = neighbours(field, q + 1, q)
-            else:
-                total = neighbours(
-                    field, q + 1, q, (early[q - 1, 0:3], early[q - 1, 3:6]),
-                    x_up=q == 2, x_down=q == 1, flat=False,
-                )
-            half = relaxed(field, q + 1, total, weight)
-            re, im = adjoint_times(lambda ri, a, b: link_t[q, ri, a, b], half)
-            turned[q, 0:3] = re
-            turned[q, 3:6] = im
+        for side, place, begun, came, planes in (
+            (0, 0, low_src, recv_low, (0, 1)),
+            (1, 4, high_src, recv_high, (3, 2)),
+        ):
+            for late_by in range(slots):
+
+                @pl.when(n == 2 * late_by)
+                def _():
+                    source_halos[late_by][side].wait_recv()
+
+            @pl.when(r > 0)
+            def _():
+                hop(side, after, r - 1, j).wait_recv()
+
+            @pl.when(r < slots)
+            def _():
+                inject = jnp.full((16, 128), take, jnp.int32) > 0
+                for part in range(6):
+                    value = jnp.where(inject, begun[d, j, part], came[r, j, part]).astype(F32)
+                    field[place, part] = value[0:8]
+                    field[place + 1, part] = value[8:16]
+
+            @pl.when(r >= slots)
+            def _():
+                for part in range(6):
+                    value = came[r, j, part].astype(F32)
+                    field[place, part] = value[0:8]
+                    field[place + 1, part] = value[8:16]
+
+            for q in planes:
+                if q == 0 or q == 3:
+                    total = neighbours(field, q + 1, q)
+                else:
+                    total = neighbours(
+                        field, q + 1, q, (early[q - 1, 0:3], early[q - 1, 3:6]),
+                        x_up=q == 2, x_down=q == 1, flat=False,
+                    )
+                half = relaxed(field, q + 1, total, weight)
+                re, im = adjoint_times(lambda ri, a, b: link_t[q, ri, a, b], half)
+                turned[q, 0:3] = re
+                turned[q, 3:6] = im
         results = []
         for x in range(2):
             re, im = relaxed(turned, x + 1, neighbours(turned, x + 1, x + 1), weight)

time: 92 us -> 91.4 us (level)
  no operation moved by 1% of the time
where the time goes in v3:
time: 91.4 us; the launch traced here: 91.3 us
  Pallas kernels  89.9 us (98%)
    pallas_call x1, Pallas kernels, local(): lax.switch(latest, [with_slots(slots) for slots in range(1, SLOTS + 1)],...  88.7 us

profile of v3, /device:TPU:1, one launch (start us, length us, event | category | flops | bytes accessed | tf_op | source)
XLA Modules:
  0.0 91.3 jit_solution(6717434261231895015)
XLA Ops:
  0.0 1.2 %shard_map.64 = s32[1]{0:T(128)} custom-call(s32[4]{0:T(128)} %times_ref.1), custom_call_target="tpu_custom_call" | custom-call | tf_op jit(solution)/shard_map/pallas_call | solution.py:489
  1.9 88.7 %conditional.1 = (f32[8,128]{1,0:T(8,128)S(1)}) conditional(s32[]{:T(128)} %bitcast, (s32[4]{0:T(128)}, s32[2,4]{1,0:T(2,128)}, f32[2,4]{1,0:T(2,128)}, f32[2,3,3,3,16,128]{5,4,3,2,1,0:T(8,128)}, f32[2,3,3,16,128]{4,3,2,1,0:T(8,128)}, /*index=5*/bf16[2,128,3,16,128]{4,3,2,1,0:T(8,128)(2,1)}) %tuple.38, (s32[4]{0:T(128)}, ...), branch_computations={%region_0.0_spmd, %region_1.0_spmd, %region_2.0_spmd, %region_3.0_... | conditional | bytes 8 | solution.py:495
  1.9 88.7 %branch_0_fun.1 = f32[8,128]{1,0:T(8,128)S(1)} custom-call(s32[4]{0:T(128)} %get-tuple-element.56.times_ref, s32[2,4]{1,0:T(2,128)} %get-tuple-element.58.index_ref, f32[2,4]{1,0:T(2,128)} %get-tuple-element.60.coef_ref, f32[2,3,3,3,16,128]{5,4,3,2,1,0:T(8,128)} %get-tuple-element.61.gauge_hbm, f32[2,3,3,16,128]{4,3,2,1,0:T(8,128)} %get-tuple-element.62.temporal_hbm, ...), custom_call_target="tpu_custom_call" | custom-call | tf_op jit(solution)/shard_map/cond/branch_0_fun/pallas_call | solution.py:495
  90.6 0.7 copy.12
